TPU v7x, 256 devices: a 8x8x2 block of a 8x8x16 slice. The times are simulated.
256 devices in a mesh: parts: 2 (over z), seq: 128 (over x, y, core).
Axes of the slice: x: 8, y: 8, z: 2, core: 2. Of those that a mesh axis runs over, the one named last changes fastest.
The devices are a block of a 8x8x16 slice.
Arguments:
- token_ids: int32 [4, 4], P(None, 'parts'), parts along dimension 1, may hold values from 0 to 76031
- lengths: int32 [4], P('parts'), parts along dimension 0, may hold values from 24576 to 32768, as said below
- embed_table: bfloat16 [76032, 5120], P('seq'), may hold values from -6 to 6
- attn_gain: bfloat16 [5120], replicated, may hold values from 0.25 to 1.75
- w_qkv: bfloat16 [5120, 7168], P('seq'), may hold values from -0.3125 to 0.3125
- qkv_bias: float32 [7168], replicated, may hold values from -8 to 8
- cache_keys: bfloat16 [4, 32768, 1024], P('parts', 'seq'), parts along dimension 0, may hold values from -300 to 300
- cache_values: bfloat16 [4, 32768, 1024], P('parts', 'seq'), parts along dimension 0, may hold values from -6 to 6
- w_out: bfloat16 [5120, 5120], P(None, 'seq'), may hold values from -0.078125 to 0.078125
- mlp_gain: bfloat16 [5120], replicated, may hold values from 0.25 to 1.75
- w_gate: bfloat16 [5120, 16384], P(None, 'seq'), may hold values from -0.078125 to 0.078125
- w_up: bfloat16 [5120, 16384], P(None, 'seq'), may hold values from -0.078125 to 0.078125
- w_down: bfloat16 [16384, 5120], P('seq'), may hold values from -0.1875 to 0.1875
Outputs:
- attended: bfloat16 [4, 4, 5120], P(None, 'parts'), parts along dimension 1
- layer_out: bfloat16 [4, 4, 5120], P(None, 'parts', 'seq'), parts along dimension 1
There are 2 independent parts, one for each index of `parts`. A program takes and returns all parts, laid end to end along the dimension named above; an argument that names none is the same for every part. Nothing has to cross between parts.
Inputs may be any that keep to these rules, and one draw needn't show every extreme that they name: Cache positions lengths[b] and later are unused; the first prompt fills the whole cache of 32768 positions.
All inputs are finite; a program needn't handle non-finite values.
Results may differ from a plain program's by a relative error of at most 0.017.
The roundings to bfloat16 on the way count: a program that leaves them out, or rounds other values in their place, can miss the bound.
Values may be sent and summed in bfloat16 or wider, within the bound.
No kernel may reach another device: no remote copies, remote signals or barrier semaphores. Data moves between devices by JAX's collectives and lax.ppermute only.
A program may use at most 128 MiB of HBM per device.

v0:
```python
import math
import jax
import jax.numpy as jnp
from jax import lax
from jax.sharding import Mesh
from jax.sharding import PartitionSpec as P

HEADS = 40
KV_HEADS = 8
HEAD_DIM = 128
SEQ = ("seq_0", "seq_1", "seq_2")
NORM_EPS = 1e-06
ROPE_BASE = 1000000.0
MASKED = -1e30


def gathered_once(array, axis):
    leaves = jax.tree.leaves(array)
    order = sorted(range(len(leaves)), key=lambda k: -leaves[k].size)
    width = (1, *leaves[order[0]].shape)[-1]
    lines = [
        jnp.pad(leaves[k].reshape(-1), (0, -leaves[k].size % width)).reshape(-1, width)
        for k in order
    ]
    both, at, found = (lax.all_gather(jnp.concatenate(lines), axis), 0, {})
    for k, line in zip(order, lines):
        slab = both[:, at : at + len(line)].reshape(len(both), -1)
        found[k] = slab[:, : leaves[k].size].reshape(-1, *leaves[k].shape)
        at += len(line)
    numbers = iter(range(len(leaves)))
    return jax.tree.map(lambda _: found[next(numbers)], array)


def combined_by_axis(array, axes, combine):
    for axis in axes:
        pieces = gathered_once(array, axis)
        array = jax.tree.map(lambda part: part[0], pieces)
        for k in range(1, lax.axis_size(axis)):
            array = combine(array, jax.tree.map(lambda part: part[k], pieces))
    return array


def sum_in_order(parts, axes, order):
    dims = [lax.axis_size(a) for a in axes]
    parts = parts.reshape(*dims, *parts.shape[1:])
    parts = parts.transpose(*order, *range(len(axes), parts.ndim))
    parts = parts.reshape(-1, *parts.shape[len(axes) :])
    for k in order:
        parts = lax.psum_scatter(parts, axes[k], scatter_dimension=0, tiled=True)
    return parts[0]


def cut_along(array, dim, devices):
    before, after = (array.shape[:dim], array.shape[dim + 1 :])
    return jnp.moveaxis(array.reshape(*before, devices, -1, *after), dim, 0)


def scatter_axes(array, axes, order, dim):
    devices = lax.axis_size(axes)
    return sum_in_order(cut_along(array, dim, devices), axes, order)


def rms_normalize(rows, gain):
    mean_square = jnp.mean(rows * rows, axis=-1, keepdims=True)
    return (rows * lax.rsqrt(mean_square + NORM_EPS) * gain.astype(jnp.float32)).astype(
        jnp.bfloat16
    )


def rotate(vectors, positions):
    half_dim = vectors.shape[-1] // 2
    frequency = ROPE_BASE ** (-2.0 * jnp.arange(half_dim, dtype=jnp.float32) / vectors.shape[-1])
    angles = positions.astype(jnp.float32)[..., None, None] * frequency
    cosine = jnp.cos(angles)
    sine_part = jnp.sin(angles)
    widened = vectors.astype(jnp.float32)
    first_half = widened[..., :half_dim]
    second = widened[..., half_dim:]
    joined = jnp.concatenate(
        [first_half * cosine - second * sine_part, second * cosine + first_half * sine_part],
        axis=-1,
    )
    return joined.astype(jnp.bfloat16)


def combine_partials(earlier, latter):
    top_one, total_one, sum_one = earlier
    top_two, total_two, sum_two = latter
    joined_top = jnp.maximum(top_one, top_two)
    scale_one = jnp.exp(top_one - joined_top)
    scale_two = jnp.exp(top_two - joined_top)
    return (
        joined_top,
        total_one * scale_one + total_two * scale_two,
        sum_one * scale_one[..., None] + sum_two * scale_two[..., None],
    )


def body(
    token_ids,
    lengths,
    embed_table,
    attn_gain,
    w_qkv,
    qkv_bias,
    cache_keys,
    cache_values,
    w_out,
    mlp_gain,
    w_gate,
    w_up,
    w_down,
):
    rank = lax.axis_index(SEQ)
    step_count, batch_count = token_ids.shape
    model_width = embed_table.shape[1]
    vocab_rows = embed_table.shape[0]
    query_width = HEADS * HEAD_DIM
    key_width = KV_HEADS * HEAD_DIM
    group_size = HEADS // KV_HEADS
    local_ids = token_ids - rank * vocab_rows
    inside = (local_ids >= 0) & (local_ids < vocab_rows)
    picked = jnp.take(embed_table, jnp.clip(local_ids, 0, vocab_rows - 1), axis=0)
    partial_rows = jnp.where(inside[..., None], picked.astype(jnp.float32), 0.0)
    stream = lax.psum(partial_rows, SEQ)
    normed = rms_normalize(stream, attn_gain).reshape(-1, model_width)
    feature_rows = w_qkv.shape[0]
    normed_local = lax.dynamic_slice_in_dim(normed, rank * feature_rows, feature_rows, 1)
    joint_partial = jnp.dot(normed_local, w_qkv, preferred_element_type=jnp.float32)
    joint_summed = lax.psum(joint_partial, SEQ)
    joint = (joint_summed + qkv_bias).astype(jnp.bfloat16).reshape(step_count, batch_count, -1)
    query_part = joint[..., :query_width].reshape(step_count, batch_count, HEADS, HEAD_DIM)
    key_part = joint[..., query_width : query_width + key_width].reshape(
        step_count, batch_count, KV_HEADS, HEAD_DIM
    )
    value_part = joint[..., query_width + key_width :].reshape(
        step_count, batch_count, KV_HEADS, HEAD_DIM
    )
    positions = lengths[None, :] + jnp.arange(step_count, dtype=jnp.int32)[:, None]
    queries = rotate(query_part, positions)
    new_keys = rotate(key_part, positions)
    grouped = queries.reshape(step_count, batch_count, KV_HEADS, group_size, HEAD_DIM)
    score_scale = 1.0 / math.sqrt(HEAD_DIM)
    local_len = cache_keys.shape[1]
    key_blocks = cache_keys.reshape(batch_count, local_len, KV_HEADS, HEAD_DIM)
    value_blocks = cache_values.reshape(batch_count, local_len, KV_HEADS, HEAD_DIM)
    scores = (
        jnp.einsum("sbkgd,bpkd->bkgsp", grouped, key_blocks, preferred_element_type=jnp.float32)
        * score_scale
    )
    places = rank * local_len + jnp.arange(local_len, dtype=jnp.int32)
    valid = (places[None, :] < lengths[:, None])[:, None, None, None, :]
    masked = jnp.where(valid, scores, MASKED)
    local_top = jnp.max(masked, axis=-1)
    weights = jnp.where(valid, jnp.exp(masked - local_top[..., None]), 0.0)
    local_total = jnp.sum(weights, axis=-1)
    local_sum = jnp.einsum(
        "bkgsp,bpkd->bkgsd",
        weights.astype(jnp.bfloat16),
        value_blocks,
        preferred_element_type=jnp.float32,
    )
    merged_top, merged_total, merged_sum = combined_by_axis(
        (local_top, local_total, local_sum), SEQ, combine_partials
    )
    new_scores = (
        jnp.einsum("sbkgd,tbkd->bkgst", grouped, new_keys, preferred_element_type=jnp.float32)
        * score_scale
    )
    step_index = jnp.arange(step_count, dtype=jnp.int32)
    causal = step_index[:, None] >= step_index[None, :]
    new_masked = jnp.where(causal, new_scores, MASKED)
    final_top = jnp.maximum(merged_top, jnp.max(new_masked, axis=-1))
    rescale = jnp.exp(merged_top - final_top)
    new_weights = jnp.where(causal, jnp.exp(new_masked - final_top[..., None]), 0.0)
    final_total = merged_total * rescale + jnp.sum(new_weights, axis=-1)
    final_sum = merged_sum * rescale[..., None] + jnp.einsum(
        "bkgst,tbkd->bkgsd",
        new_weights.astype(jnp.bfloat16),
        value_part,
        preferred_element_type=jnp.float32,
    )
    attended = jnp.transpose(final_sum / final_total[..., None], (3, 0, 1, 2, 4))
    attended = attended.reshape(step_count, batch_count, query_width).astype(jnp.bfloat16)
    shard_cols = w_out.shape[1]
    projected = jnp.dot(
        attended.reshape(-1, query_width), w_out, preferred_element_type=jnp.float32
    )
    stream_shard = lax.dynamic_slice_in_dim(stream, rank * shard_cols, shard_cols, 2)
    mid_shard = stream_shard + projected.reshape(step_count, batch_count, shard_cols)
    mid_rows = lax.all_gather(mid_shard, SEQ, axis=2, tiled=True)
    normed_mid = rms_normalize(mid_rows, mlp_gain)
    flat_rows = normed_mid.reshape(-1, model_width)
    gate = jnp.dot(flat_rows, w_gate, preferred_element_type=jnp.float32)
    upper = jnp.dot(flat_rows, w_up, preferred_element_type=jnp.float32)
    hidden = (jax.nn.silu(gate) * upper).astype(jnp.bfloat16)
    down_terms = jnp.dot(hidden, w_down, preferred_element_type=jnp.float32).reshape(
        step_count, batch_count, model_width
    )
    summed = scatter_axes(down_terms, SEQ, (2, 1, 0), 2)
    layer_out = (mid_shard + summed).astype(jnp.bfloat16)
    return (attended, layer_out)


def solution(mesh):
    finer = Mesh(
        mesh.devices.reshape(mesh.shape["parts"], 8, 8, 2), ("parts", "seq_0", "seq_1", "seq_2")
    )
    return jax.shard_map(
        body,
        mesh=finer,
        in_specs=(
            P(None, "parts"),
            P("parts"),
            P(SEQ, None),
            P(),
            P(SEQ, None),
            P(),
            P("parts", SEQ, None),
            P("parts", SEQ, None),
            P(None, SEQ),
            P(),
            P(None, SEQ),
            P(None, SEQ),
            P(SEQ, None),
        ),
        out_specs=(P(None, "parts", None), P(None, "parts", SEQ)),
        check_vma=False,
    )
```

profile of v0, /device:TPU:528, one launch (start us, length us, event | category | flops | bytes accessed | tf_op | source)
XLA Modules:
  0.0 717.2 jit_solution(17745230185070453889)
XLA Ops:
  7.3 0.8 compare_and_fusion
  8.3 4.2 gather_fusion
  12.8 0.8 convert_select_fusion
  14.4 1.1 copy-done.3
  15.8 1.1 bitcast_bitcast_fusion
  16.9 195.6 %all-reduce.14.cloned.1.call-done = f32[4,2,5120]{2,1,0:T(2,128)} async-done(((f32[4,2,5120]{2,1,0:T(2,128)}), f32[4,2,5120]{2,1,0:T(2,128)}) %all-reduce.14.cloned.1.call-update) | async-done | bytes 163856 | tf_op jit(solution)/shard_map/psum | solution.py:125
  212.4 1.1 multiply_reduce_fusion.1
  213.5 1.1 multiply_convert_fusion.1
  214.6 1.0 fusion.77
  215.8 181.4 %all-reduce.16.cloned.1.call-done = f32[8,7168]{1,0:T(8,128)} async-done(((f32[8,7168]{1,0:T(8,128)}), f32[8,7168]{1,0:T(8,128)}) %all-reduce.16.cloned.1.call-update) | async-done | bytes 229392 | tf_op jit(solution)/shard_map/psum | solution.py:130
  397.2 1.0 add_convert_fusion
  400.1 1.5 fusion.9
  402.4 38.6 %all-gather.9.cloned.1.call-done = f32[8,326,128]{2,1,0:T(8,128)} async-done(((f32[1,326,128]{2,1,0:T(8,128)}), f32[8,326,128]{2,1,0:T(8,128)}) %all-gather.9.cloned.1.call-update) | async-done | bytes 1335312 | tf_op jit(solution)/shard_map/all_gather | solution.py:25
  441.0 0.8 fusion.88
  442.1 2.0 fusion.39
  444.1 0.7 maximum_bitcast_fusion.1
  445.1 0.8 fusion.93
  446.0 38.5 %all-gather.11.cloned.1.call-done = f32[8,326,128]{2,1,0:T(8,128)} async-done(((f32[1,326,128]{2,1,0:T(8,128)}), f32[8,326,128]{2,1,0:T(8,128)}) %all-gather.11.cloned.1.call-update) | async-done | bytes 1335312 | tf_op jit(solution)/shard_map/all_gather | solution.py:25
  484.5 0.8 fusion.87
  485.6 2.0 fusion.18
  487.6 2.1 all-gather.5
  492.8 1.0 convolution_add_fusion.1
  493.9 56.9 %all_gather.27 = f32[4,2,5120]{0,1,2:T(2,128)} all-gather(f32[4,2,40]{0,1,2:T(2,128)S(1)} %copy.230), channel_id=1, replica_groups=mesh['parts'=2,'seq_0'=8,'seq_1'=8,'seq_2'=2] {'seq_0','seq_1','seq_2'}, dimensions={2}, use_global_device_ids=true | all-gather | bytes 165120 | tf_op jit(solution)/shard_map/all_gather | solution.py:191
  550.8 5.6 copy.233
  556.5 7.0 multiply_reduce_fusion
  564.2 1.9 fusion.8
  566.7 1.1 copy.236
  569.3 30.1 %all-reduce.18.cloned.1.call-done = f32[128,4,2,40]{3,1,2,0:T(4,128)} async-done(((f32[128,4,2,40]{3,1,2,0:T(4,128)}), f32[128,4,2,40]{3,1,2,0:T(4,128)}) %all-reduce.18.cloned.1.call-update) | async-done | bytes 163856
  599.4 1.7 constant_dynamic-slice_fusion.2
  603.0 75.6 %all-reduce.20.cloned.1.call-done = f32[64,4,2,40]{3,1,2,0:T(4,128)} async-done(((f32[64,4,2,40]{3,1,2,0:T(4,128)}), f32[64,4,2,40]{3,1,2,0:T(4,128)}) %all-reduce.20.cloned.1.call-update) | async-done | bytes 81936
  678.7 0.8 constant_dynamic-slice_fusion.1
  679.4 29.7 %all-reduce.8 = f32[8,4,2,40]{3,1,2,0:T(4,128)S(1)} all-reduce(f32[8,4,2,40]{3,1,2,0:T(4,128)S(1)} %constant_dynamic-slice_fusion.1), channel_id=7, replica_groups=mesh['parts'=2,'seq_0'=8,'seq_1'=8,'seq_2'=2] {'seq_0'}, use_global_device_ids=true, to_apply=%region_10.11.clone | all-reduce | flops 2560 | bytes 20480
  (137 shorter events, 12.8 us)
Async XLA Ops:
  7.2 557.1 %copy-start = (bf16[128,5120]{1,0:T(8,128)(2,1)S(1)}, bf16[128,5120]{1,0:T(8,128)(2,1)}, u32[]{:S(2)}) copy-start(bf16[128,5120]{1,0:T(8,128)(2,1)} %param.25) | copy-start | bytes 3932164
  7.2 6.6 copy-start.7
  7.2 6.6 copy-start.9
  7.2 6.8 copy-start.2
  7.2 205.2 %all-reduce.14.cloned.1.call-start = ((), (), s32[]{:S(2)}) async-start(), calls=%async_computation | async-start | bytes 327680 | tf_op jit(solution)/shard_map/psum | solution.py:125
  13.7 383.5 %all-reduce.16.cloned.1.call-start = ((), (), s32[]{:S(2)}) async-start(), calls=%async_computation.1 | async-start | bytes 458752 | tf_op jit(solution)/shard_map/psum | solution.py:130
  14.3 1.2 copy-start.3
  15.8 198.8 %copy-start.4 = (bf16[40,7168]{1,0:T(8,128)(2,1)S(1)}, bf16[40,7168]{1,0:T(8,128)(2,1)}, u32[]{:S(2)}) copy-start(bf16[40,7168]{1,0:T(8,128)(2,1)} %param.17) | copy-start | bytes 1720324
  16.9 380.3 %copy-start.6 = (f32[7168]{0:T(1024)S(1)}, f32[7168]{0:T(1024)}, u32[]{:S(2)}) copy-start(f32[7168]{0:T(1024)} %param.18) | copy-start | bytes 86020
  215.7 225.3 %all-gather.9.cloned.1.call-start = ((), (), s32[]{:S(2)}) async-start(), calls=%async_computation.2 | async-start | bytes 1511424 | tf_op jit(solution)/shard_map/all_gather | solution.py:25
  402.3 42.6 %copy-start.8 = (bf16[5120]{0:T(1024)(128)(2,1)S(1)}, bf16[5120]{0:T(1024)(128)(2,1)}, u32[]{:S(2)}) copy-start(bf16[5120]{0:T(1024)(128)(2,1)} %param.22) | copy-start | bytes 30724
  402.3 82.2 %all-gather.11.cloned.1.call-start = ((), (), s32[]{:S(2)}) async-start(), calls=%async_computation.3 | async-start | bytes 1511424 | tf_op jit(solution)/shard_map/all_gather | solution.py:25
  444.8 154.6 %all-reduce.18.cloned.1.call-start = ((), (), s32[]{:S(2)}) async-start(), calls=%async_computation.4 | async-start | bytes 1048576
  491.8 1.0 copy-start.10
  492.8 58.0 %copy-start.5 = (bf16[4,2,5120]{2,1,0:T(2,128)(2,1)}, bf16[4,2,5120]{2,1,0:T(2,128)(2,1)S(1)}, u32[]{:S(2)}) copy-start(bf16[4,2,5120]{2,1,0:T(2,128)(2,1)S(1)} %convert_element_type.84) | copy-start | bytes 245764
  556.5 7.5 %copy-start.1 = (bf16[5120,128]{1,0:T(8,128)(2,1)S(1)}, bf16[5120,128]{1,0:T(8,128)(2,1)}, u32[]{:S(2)}) copy-start(bf16[5120,128]{1,0:T(8,128)(2,1)} %param.23) | copy-start | bytes 3932164
  566.5 1.5 copy-start.13
  566.7 34.4 %copy-start.12 = (u32[256]{0:T(256)S(1)}, u32[256]{0:T(256)}, u32[]{:S(2)}) copy-start(u32[256]{0:T(256)} %constant.90) | copy-start | bytes 3076
  566.7 35.0 %copy-start.11 = (u32[256]{0:T(256)S(1)}, u32[256]{0:T(256)}, u32[]{:S(2)}) copy-start(u32[256]{0:T(256)} %constant.94) | copy-start | bytes 3076
  567.9 110.7 %all-reduce.20.cloned.1.call-start = ((), (), s32[]{:S(2)}) async-start(), calls=%async_computation.5 | async-start | bytes 524288
Sparse Core Ops, SparseCore 0:
  13.8 198.6 all-reduce.13
  215.8 181.3 all-reduce.15
  402.5 38.5 all-gather.8
  444.9 39.5 all-gather.10
  568.1 31.3 all-reduce.17
  601.6 77.0 all-reduce.19
where the time goes:
time: 718 us; the launch traced here: 717 us
  waiting for transfers between devices  560 us (78%)
  blocking collectives  88.7 us (12%)
  local copies, waits for them, and re-layouts  25.4 us (4%)
  other arithmetic  19.2 us (3%)
  between operations  16 us (2%)
  matrix products  7.37 us (1%)
    psum x1, waiting for transfers between devices, body(): stream = lax.psum(partial_rows, SEQ)  196 us
    psum x1, waiting for transfers between devices, body(): joint_summed = lax.psum(joint_partial, SEQ)  181 us
    unnamed x8, waiting for transfers between devices  106 us
    all_gather x2, waiting for transfers between devices, gathered_once(): both, at, found = (lax.all_gather(jnp.concatenate(lines), axis), 0, {})  77.1 us
    all_gather x1, blocking collectives, body(): mid_rows = lax.all_gather(mid_shard, SEQ, axis=2, tiled=True)  56.9 us
    unnamed x1, blocking collectives  29.7 us
  transfers between devices with their start and end apart: 6, of which 6 were waited for; matrix products, arithmetic and copies ran while one was open for 1% of the time, Pallas kernels for 0%

commit v1 on v0

--- a/solution.py
+++ b/solution.py
@@ -122,7 +122,8 @@
     inside = (local_ids >= 0) & (local_ids < vocab_rows)
     picked = jnp.take(embed_table, jnp.clip(local_ids, 0, vocab_rows - 1), axis=0)
     partial_rows = jnp.where(inside[..., None], picked.astype(jnp.float32), 0.0)
-    stream = lax.psum(partial_rows, SEQ)
+    shards = lax.all_gather(partial_rows, SEQ, axis=0, tiled=False)
+    stream = shards.sum(axis=0)
     normed = rms_normalize(stream, attn_gain).reshape(-1, model_width)
     feature_rows = w_qkv.shape[0]
     normed_local = lax.dynamic_slice_in_dim(normed, rank * feature_rows, feature_rows, 1)

time: 718 us -> 648 us (0.903)
  waiting for transfers between devices: 560 us -> 484 us
    psum x1 -> x0, waiting for transfers between devices: 196 us -> none  [body(): stream = lax.psum(partial_rows, SEQ)]
    all_gather x0 -> x1, waiting for transfers between devices: none -> 117 us  [body(): shards = lax.all_gather(partial_rows, SEQ, axis=0, tiled=False)]
    reduce_sum x0 -> x1, other arithmetic: none -> 10.9 us  [body(): stream = shards.sum(axis=0)]
    reduce_sum x2, other arithmetic: 8.13 us -> 0.28 us  [rms_normalize(): mean_square = jnp.mean(rows * rows, axis=-1, keepdims=True)]
where the time goes in v1:
time: 648 us; the launch traced here: 647 us
  waiting for transfers between devices  484 us (75%)
  blocking collectives  88.7 us (14%)
  local copies, waits for them, and re-layouts  28.5 us (4%)
  other arithmetic  21.2 us (3%)
  between operations  16 us (2%)
  matrix products  7.73 us (1%)
    psum x1, waiting for transfers between devices, body(): joint_summed = lax.psum(joint_partial, SEQ)  184 us
    all_gather x1, waiting for transfers between devices, body(): shards = lax.all_gather(partial_rows, SEQ, axis=0, tiled=False)  117 us
    unnamed x8, waiting for transfers between devices  106 us
    all_gather x2, waiting for transfers between devices, gathered_once(): both, at, found = (lax.all_gather(jnp.concatenate(lines), axis), 0, {})  77.1 us
    all_gather x1, blocking collectives, body(): mid_rows = lax.all_gather(mid_shard, SEQ, axis=2, tiled=True)  56.9 us
    unnamed x1, blocking collectives  29.7 us
  transfers between devices with their start and end apart: 6, of which 6 were waited for; matrix products, arithmetic and copies ran while one was open for 1% of the time, Pallas kernels for 0%

profile of v1, /device:TPU:528, one launch (start us, length us, event | category | flops | bytes accessed | tf_op | source)
XLA Modules:
  0.0 646.9 jit_solution(978731221250273729)
XLA Ops:
  7.3 0.8 compare_and_fusion
  8.3 4.2 gather_fusion
  12.6 0.8 convert_select_fusion
  13.7 1.3 copy.196
  15.0 1.5 copy.197
  16.5 0.8 dynamic-slice.6
  17.2 1.3 bitcast_bitcast_fusion.1
  18.5 1.0 bitcast_bitcast_fusion
  19.6 117.1 %all-gather.10.cloned.1.call-done = f32[128,4,2,5120]{3,1,2,0:T(4,128)} async-done(((f32[1,4,2,5120]{3,1,2,0:T(4,128)}), f32[128,4,2,5120]{3,1,2,0:T(4,128)}) %all-gather.10.cloned.1.call-update) | async-done | bytes 20971536 | tf_op jit(solution)/shard_map/all_gather | solution.py:125
  136.7 10.9 %reduce_sum.47 = f32[4,2,5120]{2,0,1:T(4,128)S(1)} reduce(f32[128,4,2,5120]{3,1,2,0:T(4,128)} %all-gather.10.cloned.1.call-done, f32[]{:T(128)} %constant.18.clone.1), dimensions={0}, to_apply=%region_0.1 | reduce | flops 5201920 | bytes 21135364 | tf_op jit(solution)/shard_map/reduce_sum | solution.py:126
  148.2 2.0 fusion.78
  150.4 184.2 %all-reduce.13.cloned.1.call-done = f32[8,7168]{1,0:T(8,128)} async-done(((f32[8,7168]{1,0:T(8,128)}), f32[8,7168]{1,0:T(8,128)}) %all-reduce.13.cloned.1.call-update) | async-done | bytes 229392 | tf_op jit(solution)/shard_map/psum | solution.py:131
  334.6 1.0 add_convert_fusion
  337.5 1.5 fusion.9
  339.8 38.6 %all-gather.12.cloned.1.call-done = f32[8,326,128]{2,1,0:T(8,128)} async-done(((f32[1,326,128]{2,1,0:T(8,128)}), f32[8,326,128]{2,1,0:T(8,128)}) %all-gather.12.cloned.1.call-update) | async-done | bytes 1335312 | tf_op jit(solution)/shard_map/all_gather | solution.py:25
  378.4 0.8 fusion.92
  379.5 2.0 fusion.39
  381.5 0.7 maximum_bitcast_fusion.1
  382.5 0.8 fusion.97
  383.5 38.5 %all-gather.14.cloned.1.call-done = f32[8,326,128]{2,1,0:T(8,128)} async-done(((f32[1,326,128]{2,1,0:T(8,128)}), f32[8,326,128]{2,1,0:T(8,128)}) %all-gather.14.cloned.1.call-update) | async-done | bytes 1335312 | tf_op jit(solution)/shard_map/all_gather | solution.py:25
  421.9 0.8 fusion.91
  423.0 2.0 fusion.18
  425.0 2.1 all-gather.5
  430.6 56.9 %all_gather.32 = f32[4,2,5120]{0,1,2:T(2,128)} all-gather(f32[4,2,40]{0,1,2:T(2,128)S(1)} %copy.169), channel_id=1, replica_groups=mesh['parts'=2,'seq_0'=8,'seq_1'=8,'seq_2'=2] {'seq_0','seq_1','seq_2'}, dimensions={2}, use_global_device_ids=true | all-gather | bytes 165120 | tf_op jit(solution)/shard_map/all_gather | solution.py:192
  487.5 5.8 copy.172
  494.0 1.9 fusion.8
  496.5 1.1 copy.175
  499.0 30.1 %all-reduce.15.cloned.1.call-done = f32[128,4,2,40]{3,1,2,0:T(4,128)} async-done(((f32[128,4,2,40]{3,1,2,0:T(4,128)}), f32[128,4,2,40]{3,1,2,0:T(4,128)}) %all-reduce.15.cloned.1.call-update) | async-done | bytes 163856
  529.1 1.7 constant_dynamic-slice_fusion.2
  532.8 75.6 %all-reduce.17.cloned.1.call-done = f32[64,4,2,40]{3,1,2,0:T(4,128)} async-done(((f32[64,4,2,40]{3,1,2,0:T(4,128)}), f32[64,4,2,40]{3,1,2,0:T(4,128)}) %all-reduce.17.cloned.1.call-update) | async-done | bytes 81936
  608.4 0.8 constant_dynamic-slice_fusion.1
  609.2 29.7 %all-reduce.8 = f32[8,4,2,40]{3,1,2,0:T(4,128)S(1)} all-reduce(f32[8,4,2,40]{3,1,2,0:T(4,128)S(1)} %constant_dynamic-slice_fusion.1), channel_id=7, replica_groups=mesh['parts'=2,'seq_0'=8,'seq_1'=8,'seq_2'=2] {'seq_0'}, use_global_device_ids=true, to_apply=%region_10.11.clone | all-reduce | flops 2560 | bytes 20480
  (130 shorter events, 12.7 us)
Async XLA Ops:
  7.2 486.8 %copy-start = (bf16[128,5120]{1,0:T(8,128)(2,1)S(1)}, bf16[128,5120]{1,0:T(8,128)(2,1)}, u32[]{:S(2)}) copy-start(bf16[128,5120]{1,0:T(8,128)(2,1)} %param.25) | copy-start | bytes 3932164
  7.2 6.3 copy-start.6
  7.2 6.5 %copy-start.2 = (bf16[2,256,1024]{2,1,0:T(8,128)(2,1)S(1)}, bf16[2,256,1024]{2,1,0:T(8,128)(2,1)}, u32[]{:S(2)}) copy-start(bf16[2,256,1024]{2,1,0:T(8,128)(2,1)} %param.19) | copy-start | bytes 3145732
  7.2 129.4 %all-gather.10.cloned.1.call-start = ((), (), s32[]{:S(2)}) async-start(), calls=%async_computation | async-start | bytes 21135360 | tf_op jit(solution)/shard_map/all_gather | solution.py:125
  13.4 321.2 %all-reduce.13.cloned.1.call-start = ((), (), s32[]{:S(2)}) async-start(), calls=%async_computation.1 | async-start | bytes 458752 | tf_op jit(solution)/shard_map/psum | solution.py:131
  147.6 187.0 %copy-start.4 = (f32[7168]{0:T(1024)S(1)}, f32[7168]{0:T(1024)}, u32[]{:S(2)}) copy-start(f32[7168]{0:T(1024)} %param.18) | copy-start | bytes 86020
  150.3 228.1 %all-gather.12.cloned.1.call-start = ((), (), s32[]{:S(2)}) async-start(), calls=%async_computation.2 | async-start | bytes 1511424 | tf_op jit(solution)/shard_map/all_gather | solution.py:25
  339.7 42.6 %copy-start.5 = (bf16[5120]{0:T(1024)(128)(2,1)S(1)}, bf16[5120]{0:T(1024)(128)(2,1)}, u32[]{:S(2)}) copy-start(bf16[5120]{0:T(1024)(128)(2,1)} %param.22) | copy-start | bytes 30724
  339.8 82.2 %all-gather.14.cloned.1.call-start = ((), (), s32[]{:S(2)}) async-start(), calls=%async_computation.3 | async-start | bytes 1511424 | tf_op jit(solution)/shard_map/all_gather | solution.py:25
  382.2 146.9 %all-reduce.15.cloned.1.call-start = ((), (), s32[]{:S(2)}) async-start(), calls=%async_computation.4 | async-start | bytes 1048576
  429.2 1.0 copy-start.7
  430.2 57.3 %copy-start.3 = (bf16[4,2,5120]{2,1,0:T(2,128)(2,1)}, bf16[4,2,5120]{2,1,0:T(2,128)(2,1)S(1)}, u32[]{:S(2)}) copy-start(bf16[4,2,5120]{2,1,0:T(2,128)(2,1)S(1)} %convert_element_type.92) | copy-start | bytes 245764
  487.5 6.1 copy-start.1
  496.3 1.5 copy-start.10
  496.4 34.4 %copy-start.9 = (u32[256]{0:T(256)S(1)}, u32[256]{0:T(256)}, u32[]{:S(2)}) copy-start(u32[256]{0:T(256)} %constant.90) | copy-start | bytes 3076
  496.4 35.0 %copy-start.8 = (u32[256]{0:T(256)S(1)}, u32[256]{0:T(256)}, u32[]{:S(2)}) copy-start(u32[256]{0:T(256)} %constant.94) | copy-start | bytes 3076
  497.7 110.7 %all-reduce.17.cloned.1.call-start = ((), (), s32[]{:S(2)}) async-start(), calls=%async_computation.5 | async-start | bytes 524288
Sparse Core Ops, SparseCore 0:
  13.5 123.0 all-gather.9
  150.4 184.1 all-reduce.12
  339.9 38.5 all-gather.11
  382.3 39.5 all-gather.13
  497.8 31.3 all-reduce.14
  531.3 77.0 all-reduce.16
